TPU v7x, 32 devices: a whole 2x2x4 slice. The times are simulated.
32 devices in a mesh: seq: 8 (over z, x), head: 4 (over y, core).
Axes of the slice: x: 2, y: 2, z: 4, core: 2. Of those that a mesh axis runs over, the one named last changes fastest.
Arguments:
- queries: bfloat16 [8192, 2048], P('seq', 'head'), may hold values from -200 to 200
- keys: bfloat16 [8192, 2048], P('seq', 'head'), may hold values from -6 to 6
- values: bfloat16 [8192, 2048], P('seq', 'head'), may hold values from -12 to 12
- gate_bias: float32 [16], P('head'), may hold values from -2 to 2
- out_weight: bfloat16 [2048, 4096], P(None, 'head'), may hold values from -0.125 to 0.125
Outputs:
- layer_out: bfloat16 [8192, 4096], P('seq', 'head')
All inputs are finite; a program needn't handle non-finite values.
Results may differ from a plain program's by a relative error of at most 0.007.
Values may be sent and summed in bfloat16 or wider, within the bound.
A program may use at most 128 MiB of HBM per device.

v0:
```python
import functools

import jax
import jax.numpy as jnp
from jax import lax
from jax.experimental import pallas as pl
from jax.experimental.pallas import tpu as pltpu
from jax.sharding import PartitionSpec as P

DH = 128
SEG = 256
MEM = DH + 8
PAIR = 2 * DH
MESH = pl.DeviceIdType.MESH
F32 = jnp.float32
BF16 = jnp.bfloat16
NT = (((1,), (1,)), ((), ()))
TN = (((0,), (0,)), ((), ()))


def elu1(x):
    return jnp.where(x > 0.0, x + 1.0, jnp.exp(jnp.minimum(x, 0.0)))


def split(x):
    top = x.astype(BF16)
    return top, (x - top.astype(F32)).astype(BF16)


def kernel(
    ns, nh, q_ref, k_ref, v_ref, gate_ref, w_hbm, out_ref,
    w_ref, local, inner, total, from_pair, from_prev, to_next, prior, ctx, acc,
    w_sem, x_send, x_recv, z_send, z_recv, c_send, c_recv, f_send,
):
    rows, cols = q_ref.shape
    segs, heads = rows // SEG, cols // DH
    pairs = heads // 2
    blocks = segs * heads
    me_s, me_h = lax.axis_index("seq"), lax.axis_index("head")
    z, odd = me_s // 2, lax.rem(me_s, 2)
    zs = ns // 2
    pair_s = me_s + 1 - 2 * odd
    up, down = lax.rem(me_s + 2, ns), lax.rem(me_s + ns - 2, ns)
    group, core = me_h // 2, lax.rem(me_h, 2)
    pair_h = me_h + 1 - 2 * core
    groups = nh // 2

    weight_copy = pltpu.make_async_copy(w_hbm, w_ref, w_sem)
    weight_copy.start()

    barrier = pltpu.get_barrier_semaphore()
    seq_peers = [pair_s, up, down]
    for s in seq_peers:
        pl.semaphore_signal(barrier, inc=1, device_id=(s, me_h), device_id_type=MESH)
    far = [lax.rem(group + d, groups) * 2 + core for d in range(1, groups)]
    for h in [pair_h] + far:
        pl.semaphore_signal(barrier, inc=1, device_id=(me_s, h), device_id_type=MESH)

    def x_copy(h):
        return pltpu.make_async_remote_copy(
            src_ref=total.at[h], dst_ref=from_pair.at[h],
            send_sem=x_send.at[h], recv_sem=x_recv.at[h],
            device_id=(pair_s, me_h), device_id_type=MESH,
        )

    def z_copy(h):
        return pltpu.make_async_remote_copy(
            src_ref=to_next.at[h], dst_ref=from_prev.at[h],
            send_sem=z_send.at[h], recv_sem=z_recv.at[h],
            device_id=(up, me_h), device_id_type=MESH,
        )

    def ctx_copy(source, target, j, s, send):
        part = ctx.at[source * pairs + j, pl.ds(pl.multiple_of(s * SEG, SEG), SEG)]
        return pltpu.make_async_remote_copy(
            src_ref=part, dst_ref=part,
            send_sem=send, recv_sem=c_recv.at[source, j, s],
            device_id=(me_s, target), device_id_type=MESH,
        )

    for h in range(heads):
        span = pl.ds(h * DH, DH)
        run = jnp.zeros((MEM, DH), F32)
        for s in range(segs):
            inner[h, s] = run
            part = pl.ds(s * SEG, SEG)
            key_map = elu1(k_ref[part, span].astype(F32)).astype(BF16)
            delta = lax.dot_general(v_ref[part, span], key_map, TN, preferred_element_type=F32)
            norm = jnp.sum(key_map.astype(F32), axis=0, keepdims=True)
            run = run + jnp.concatenate([delta, jnp.broadcast_to(norm, (8, DH))], axis=0)
        total[h] = run
        if h == 0:
            pl.semaphore_wait(barrier, 3 + 1 + len(far))
        x_copy(h).start()

    @pl.when(z == 0)
    def _():
        from_prev[...] = jnp.zeros_like(from_prev)

    def chain(h):
        x_copy(h).wait_recv()

        @pl.when(z > 0)
        def _():
            z_copy(h).wait_recv()

        before = from_prev[h]
        other = from_pair[h]

        @pl.when(z < zs - 1)
        def _():
            to_next[h] = before + (total[h] + other)
            z_copy(h).start()

        prior[h] = before + jnp.where(odd == 1, other, 0.0)

    row_id = lax.broadcasted_iota(jnp.int32, (SEG, SEG), 0)
    col_id = lax.broadcasted_iota(jnp.int32, (SEG, SEG), 1)
    ones = jnp.ones((SEG, DH), BF16)
    first, hop = 3, 5

    @pl.loop(0, blocks)
    def _(b):
        for c in range(heads):
            @pl.when(b == first + 2 * c + hop * z)
            def _():
                chain(c)
        h, s = b // segs, lax.rem(b, segs)
        span = pl.ds(pl.multiple_of(h * DH, DH), DH)
        part = pl.ds(pl.multiple_of(s * SEG, SEG), SEG)
        scores = lax.dot_general(q_ref[part, span], k_ref[part, span], NT, preferred_element_type=F32)
        scores = jnp.where(row_id >= col_id, scores * (1.0 / DH**0.5), -1e30)
        weights = jnp.exp(scores - jnp.max(scores, axis=1, keepdims=True)).astype(BF16)
        both = jnp.dot(
            weights, jnp.concatenate([v_ref[part, span], ones], axis=1), preferred_element_type=F32
        )
        local[part, span] = both[:, :DH] / both[:, DH:]

    for c in range(heads):
        @pl.when(first + 2 * c + hop * z >= blocks)
        def _():
            chain(c)

    for j in range(pairs):
        gates = [
            1.0 / (1.0 + jnp.exp(-jnp.full((1, DH), gate_ref[2 * j + i], F32))) for i in range(2)
        ]

        @pl.loop(0, segs)
        def _(s):
            part = pl.ds(pl.multiple_of(s * SEG, SEG), SEG)
            mixed = []
            for i in range(2):
                h = 2 * j + i
                span = pl.ds(h * DH, DH)
                mem = prior[h] + inner[h, s]
                mem = jnp.concatenate(
                    [mem[:DH], jnp.broadcast_to(mem[DH : DH + 1], (DH, DH))], axis=0
                )
                m_top, m_low = split(mem)
                q_top, q_low = split(elu1(q_ref[part, span].astype(F32)))
                recall = lax.dot_general(
                    jnp.concatenate([q_top, q_low], axis=1),
                    jnp.concatenate([m_top, m_top], axis=1),
                    NT, preferred_element_type=F32,
                ) + lax.dot_general(q_top, m_low, NT, preferred_element_type=F32)
                recall = recall[:, :DH] / (recall[:, DH:] + 1.0)
                mixed.append(gates[i] * recall + (1.0 - gates[i]) * local[part, span])
            ctx[me_h * pairs + j, part] = jnp.concatenate(mixed, axis=1).astype(BF16)
            for t in far + [pair_h]:
                ctx_copy(me_h, t, j, s, c_send.at[t, j, s]).start()

    weight_copy.wait()

    def product(source, j, part):
        slot = source * pairs + j
        return jnp.dot(
            ctx[slot, part],
            w_ref[pl.ds(pl.multiple_of(slot * PAIR, PAIR), PAIR), :],
            preferred_element_type=F32,
        )

    @pl.loop(0, segs)
    def _(s):
        part = pl.ds(pl.multiple_of(s * SEG, SEG), SEG)
        for j in range(pairs):
            ctx_copy(pair_h, pair_h, j, s, c_send.at[pair_h, j, s]).wait_recv()
        sums = product(me_h, 0, part)
        for j in range(1, pairs):
            sums = sums + product(me_h, j, part)
        for j in range(pairs):
            sums = sums + product(pair_h, j, part)
        acc[part, :] = sums

    for j in range(pairs):
        for f in far:
            twin = (f // 2) * 2 + 1 - core

            @pl.loop(0, segs)
            def _(s):
                part = pl.ds(pl.multiple_of(s * SEG, SEG), SEG)
                ctx_copy(f, pair_h, j, s, c_send.at[f, j, s]).wait_recv()
                ctx_copy(f, pair_h, j, s, f_send.at[f, j, s]).start()
                sums = acc[part, :] + product(f, j, part)
                ctx_copy(twin, pair_h, j, s, c_send.at[f, j, s]).wait_recv()
                acc[part, :] = sums + product(twin, j, part)

    out_ref[...] = acc[...].astype(BF16)

    for h in range(heads):
        x_copy(h).wait_send()

        @pl.when(z < zs - 1)
        def _():
            z_copy(h).wait_send()

    for j in range(pairs):
        @pl.loop(0, segs)
        def _(s):
            for t in far + [pair_h]:
                ctx_copy(me_h, t, j, s, c_send.at[t, j, s]).wait_send()
            for f in far:
                ctx_copy(f, pair_h, j, s, f_send.at[f, j, s]).wait_send()


def body(ns, nh, queries, keys, values, gate_bias, out_weight):
    rows, cols = queries.shape
    depth, outs = out_weight.shape
    segs, heads = rows // SEG, cols // DH
    pairs = heads // 2
    vmem = pl.BlockSpec(memory_space=pltpu.VMEM)
    dma = pltpu.SemaphoreType.DMA
    mem = pltpu.VMEM((heads, MEM, DH), F32)
    return pl.pallas_call(
        functools.partial(kernel, ns, nh),
        out_shape=jax.ShapeDtypeStruct((rows, outs), BF16),
        in_specs=[vmem, vmem, vmem, pl.BlockSpec(memory_space=pltpu.SMEM),
                  pl.BlockSpec(memory_space=pl.ANY)],
        out_specs=vmem,
        scratch_shapes=[
            pltpu.VMEM((depth, outs), BF16),
            pltpu.VMEM((rows, cols), F32),
            pltpu.VMEM((heads, segs, MEM, DH), F32),
            mem, mem, mem, mem, mem,
            pltpu.VMEM((nh * pairs, rows, PAIR), BF16),
            pltpu.VMEM((rows, outs), F32),
            dma, dma((heads,)), dma((heads,)), dma((heads,)), dma((heads,)),
            dma((nh, pairs, segs)), dma((nh, pairs, segs)), dma((nh, pairs, segs)),
        ],
        compiler_params=pltpu.CompilerParams(
            collective_id=0, has_side_effects=True, vmem_limit_bytes=60 * 1024 * 1024
        ),
        name="infini_layer",
    )(queries, keys, values, gate_bias, out_weight)


def solution(mesh):
    sizes = dict(mesh.shape)
    return jax.shard_map(
        functools.partial(body, sizes["seq"], sizes["head"]),
        mesh=mesh,
        in_specs=(P("seq", "head"), P("seq", "head"), P("seq", "head"), P("head"), P(None, "head")),
        out_specs=P("seq", "head"),
        check_vma=False,
    )
```

profile of v0, /device:TPU:25, one launch (start us, length us, event | category | flops | bytes accessed | tf_op | source)
XLA Modules:
  0.0 52.5 jit_solution(7627174808739633525)
XLA Ops:
  0.0 49.4 %infini_layer.1 = bf16[1024,1024]{1,0:T(8,128)(2,1)} custom-call(bf16[1024,512]{1,0:T(8,128)(2,1)} %q_ref.1, bf16[1024,512]{1,0:T(8,128)(2,1)} %k_ref.1, bf16[1024,512]{1,0:T(8,128)(2,1)} %v_ref.1, f32[4]{0:T(128)} %gate_ref.1, bf16[2048,1024]{1,0:T(8,128)(2,1)} %w_hbm.1), custom_call_target="tpu_custom_call" | custom-call | tf_op jit(solution)/shard_map/infini_layer/pallas_call | solution.py:234
  49.4 3.1 %copy.7 = bf16[1024,1024]{1,0:T(8,128)(2,1)} copy(bf16[1024,1024]{1,0:T(8,128)(2,1)} %infini_layer.1) | data formatting | bytes 4194304
where the time goes:
time: 52.7 us; the launch traced here: 52.5 us
  Pallas kernels  49.4 us (94%)
  local copies, waits for them, and re-layouts  3.08 us (6%)
    pallas_call x1, Pallas kernels, body(): pl.pallas_call(functools.partial(kernel, ns, nh), out_shape=jax.ShapeDtyp...  49.4 us
    unnamed x1, local copies, waits for them, and re-layouts  3.08 us

commit v1 on v0

--- a/solution.py
+++ b/solution.py
@@ -233,7 +233,7 @@
     mem = pltpu.VMEM((heads, MEM, DH), F32)
     return pl.pallas_call(
         functools.partial(kernel, ns, nh),
-        out_shape=jax.ShapeDtypeStruct((rows, outs), BF16),
+        out_shape=pltpu.VMEM((rows, outs), BF16),
         in_specs=[vmem, vmem, vmem, pl.BlockSpec(memory_space=pltpu.SMEM),
                   pl.BlockSpec(memory_space=pl.ANY)],
         out_specs=vmem,

time: 52.7 us -> 49.6 us (0.941)
  local copies, waits for them, and re-layouts: 3.08 us -> 1.32 us
  Pallas kernels: 49.4 us -> 48.1 us
    unnamed x1, local copies, waits for them, and re-layouts: 3.08 us -> 1.32 us
    pallas_call x1, Pallas kernels: 49.4 us -> 48.1 us  [body(): pl.pallas_call(functools.partial(kernel, ns, nh), out_shape=pltpu.VMEM((r...]
where the time goes in v1:
time: 49.6 us; the launch traced here: 49.4 us
  Pallas kernels  48.1 us (97%)
  local copies, waits for them, and re-layouts  1.32 us (3%)
    pallas_call x1, Pallas kernels, body(): pl.pallas_call(functools.partial(kernel, ns, nh), out_shape=pltpu.VMEM((r...  48.1 us
    unnamed x1, local copies, waits for them, and re-layouts  1.32 us

profile of v1, /device:TPU:25, one launch (start us, length us, event | category | flops | bytes accessed | tf_op | source)
XLA Modules:
  0.0 49.4 jit_solution(5195068896953146019)
XLA Ops:
  0.0 48.1 %infini_layer.1 = bf16[1024,1024]{1,0:T(8,128)(2,1)S(1)} custom-call(bf16[1024,512]{1,0:T(8,128)(2,1)} %q_ref.1, bf16[1024,512]{1,0:T(8,128)(2,1)} %k_ref.1, bf16[1024,512]{1,0:T(8,128)(2,1)} %v_ref.1, f32[4]{0:T(128)} %gate_ref.1, bf16[2048,1024]{1,0:T(8,128)(2,1)} %w_hbm.1), custom_call_target="tpu_custom_call" | custom-call | tf_op jit(solution)/shard_map/infini_layer/pallas_call | solution.py:234
  48.1 1.3 %copy.7 = bf16[1024,1024]{1,0:T(8,128)(2,1)} copy(bf16[1024,1024]{1,0:T(8,128)(2,1)S(1)} %infini_layer.1) | data formatting | bytes 4194304

commit v2 on v1

v2 whole, which is shorter than its diff:
```python
import functools

import jax
import jax.numpy as jnp
from jax import lax
from jax.experimental import pallas as pl
from jax.experimental.pallas import tpu as pltpu
from jax.sharding import PartitionSpec as P

DH = 128
SEG = 256
MEM = DH + 8
SENT = DH + 16
X_FIRST = 4
CTX_FIRST = 4
CTX_HOP = 4
MESH = pl.DeviceIdType.MESH
F32 = jnp.float32
BF16 = jnp.bfloat16
NT = (((1,), (1,)), ((), ()))
TN = (((0,), (0,)), ((), ()))


def elu1(x):
    return jnp.where(x > 0.0, x + 1.0, jnp.exp(jnp.minimum(x, 0.0)))


def rows_of(s):
    return pl.ds(pl.multiple_of(s * SEG, SEG), SEG)


def kernel(
    ns, nh, q_hbm, k_hbm, v_hbm, gate_ref, w_hbm, out_ref,
    q_ref, k_ref, v_ref, w_ref, local, inner, total, mine, from_pair, plane, from_plane, prior, ctx, acc,
    in_sem, w_sem, x_send, x_recv, z_send, z_recv, c_send, c_recv, f_send,
):
    heads, rows, _ = q_ref.shape
    segs = rows // SEG
    pairs = heads // 2
    blocks = segs * heads
    me_s, me_h = lax.axis_index("seq"), lax.axis_index("head")
    z, odd = me_s // 2, lax.rem(me_s, 2)
    zs = ns // 2
    pair_s = me_s + 1 - 2 * odd
    group, core = me_h // 2, lax.rem(me_h, 2)
    pair_h = me_h + 1 - 2 * core
    groups = nh // 2

    def load(i, h):
        src, dst = ((k_hbm, k_ref), (v_hbm, v_ref), (q_hbm, q_ref))[i]
        return pltpu.make_async_copy(src.at[:, pl.ds(h * DH, DH)], dst.at[h], in_sem.at[i, h])

    weight_copy = pltpu.make_async_copy(w_hbm, w_ref, w_sem)
    for h in range(heads):
        load(0, h).start()
        load(1, h).start()
    for h in range(heads):
        load(2, h).start()
    weight_copy.start()

    barrier = pltpu.get_barrier_semaphore()
    pl.semaphore_signal(barrier, inc=1, device_id=(pair_s, me_h), device_id_type=MESH)
    for d in range(1, zs):
        peer = lax.rem(z + d, zs) * 2 + odd
        pl.semaphore_signal(barrier, inc=1, device_id=(peer, me_h), device_id_type=MESH)
    far = [lax.rem(group + d, groups) * 2 + core for d in range(1, groups)]
    for h in [pair_h] + far:
        pl.semaphore_signal(barrier, inc=1, device_id=(me_s, h), device_id_type=MESH)

    def x_copy(h):
        return pltpu.make_async_remote_copy(
            src_ref=mine.at[h], dst_ref=from_pair.at[h],
            send_sem=x_send.at[h], recv_sem=x_recv.at[h],
            device_id=(pair_s, me_h), device_id_type=MESH,
        )

    def z_copy(source, target, h):
        return pltpu.make_async_remote_copy(
            src_ref=plane.at[h], dst_ref=from_plane.at[source, h],
            send_sem=z_send.at[target, h], recv_sem=z_recv.at[source, h],
            device_id=(target * 2 + odd, me_h), device_id_type=MESH,
        )

    def ctx_copy(source, target, h, s, send):
        part = ctx.at[source * heads + h, rows_of(s)]
        return pltpu.make_async_remote_copy(
            src_ref=part, dst_ref=part,
            send_sem=send, recv_sem=c_recv.at[source, h, s],
            device_id=(me_s, target), device_id_type=MESH,
        )

    for h in range(heads):
        load(0, h).wait()
        load(1, h).wait()
        run = jnp.zeros((MEM, DH), F32)
        for s in range(segs):
            inner[h, s] = run
            part = pl.ds(s * SEG, SEG)
            key_map = elu1(k_ref[h, part].astype(F32)).astype(BF16)
            delta = lax.dot_general(v_ref[h, part], key_map, TN, preferred_element_type=F32)
            norm = jnp.sum(key_map.astype(F32), axis=0, keepdims=True)
            run = run + jnp.concatenate([delta, jnp.broadcast_to(norm, (8, DH))], axis=0)
        total[h] = run
        mine[h] = jnp.concatenate([run, run[DH:]], axis=0).astype(BF16)
        if h == 0:
            pl.semaphore_wait(barrier, zs + 1 + len(far))
        x_copy(h).start()

    for h in range(heads):
        load(2, h).wait()

    def meet(h):
        x_copy(h).wait_recv()
        other = from_pair[h].astype(F32)[:MEM]
        both = total[h] + other
        plane[h] = jnp.concatenate([both, both[DH:]], axis=0).astype(BF16)

        @pl.loop(0, zs - 1 - z)
        def _(d):
            z_copy(z, zs - 1 - d, h).start()

        prior[h] = jnp.where(odd == 1, other, 0.0)

    def mix(h, s):
        part = rows_of(s)
        gate = 1.0 / (1.0 + jnp.exp(-jnp.full((1, DH), gate_ref[h], F32)))
        mem = prior[h] + inner[h, s]
        mem = jnp.concatenate(
            [mem[:DH], jnp.broadcast_to(mem[DH : DH + 1], (DH, DH))], axis=0
        ).astype(BF16)
        q_map = elu1(q_ref[h, part].astype(F32)).astype(BF16)
        recall = lax.dot_general(q_map, mem, NT, preferred_element_type=F32)
        recall = recall[:, :DH] / (recall[:, DH:] + 1.0)
        ctx[me_h * heads + h, part] = (gate * recall + (1.0 - gate) * local[h, part]).astype(BF16)
        for t in far + [pair_h]:
            ctx_copy(me_h, t, h, s, c_send.at[t, h, s]).start()

    def arrive(h):
        @pl.loop(0, z)
        def _(p):
            z_copy(p, z, h).wait_recv()
            prior[h] = prior[h] + from_plane[p, h].astype(F32)[:MEM]

    def finish(c):
        arrive(c)
        if c < heads - 2:
            @pl.loop(0, segs)
            def _(s):
                mix(c, s)
        elif c == heads - 1:
            @pl.loop(0, segs)
            def _(s):
                mix(c - 1, s)
                mix(c, s)

    row_id = lax.broadcasted_iota(jnp.int32, (SEG, SEG), 0)
    col_id = lax.broadcasted_iota(jnp.int32, (SEG, SEG), 1)
    ones = jnp.ones((SEG, DH), BF16)

    def meet_at(c):
        return X_FIRST + c

    def finish_at(c):
        ready = CTX_FIRST + X_FIRST + CTX_HOP * jnp.minimum(z, 1) + c
        return jnp.maximum(ready, segs * (c + 1))

    @pl.loop(0, blocks)
    def _(b):
        for c in range(heads):
            @pl.when(b == meet_at(c))
            def _():
                meet(c)
        for c in range(heads):
            @pl.when(b == finish_at(c))
            def _():
                finish(c)
        h, s = b // segs, lax.rem(b, segs)
        part = rows_of(s)
        scores = lax.dot_general(q_ref[h, part], k_ref[h, part], NT, preferred_element_type=F32)
        scores = jnp.where(row_id >= col_id, scores * (1.0 / DH**0.5), -1e30)
        weights = jnp.exp(scores - jnp.max(scores, axis=1, keepdims=True)).astype(BF16)
        both = jnp.dot(
            weights, jnp.concatenate([v_ref[h, part], ones], axis=1), preferred_element_type=F32
        )
        local[h, part] = both[:, :DH] / both[:, DH:]

    for c in range(heads):
        if meet_at(c) >= blocks:
            meet(c)
    for c in range(heads):
        @pl.when(finish_at(c) >= blocks)
        def _():
            finish(c)

    weight_copy.wait()

    def product(source, j, part):
        slot = source * heads + 2 * j
        return jnp.dot(
            jnp.concatenate([ctx[slot, part], ctx[slot + 1, part]], axis=1),
            w_ref[pl.ds(pl.multiple_of(slot * DH, 2 * DH), 2 * DH), :],
            preferred_element_type=F32,
        )

    def took(source, h, s):
        ctx_copy(source, pair_h, h, s, c_send.at[pair_h, h, s]).wait_recv()

    def twin_of(f):
        return (f // 2) * 2 + 1 - core

    def relay(f, h, s):
        took(f, h, s)
        ctx_copy(f, pair_h, h, s, f_send.at[f, h, s]).start()

    @pl.loop(0, segs)
    def _(s):
        part = rows_of(s)
        for h in range(heads):
            took(pair_h, h, s)
        sums = product(me_h, 0, part)
        for j in range(1, pairs):
            sums = sums + product(me_h, j, part)
        for j in range(pairs):
            sums = sums + product(pair_h, j, part)
        acc[part, :] = sums

    for j in range(pairs - 1):
        for h in (2 * j, 2 * j + 1):
            for f in far:
                @pl.loop(0, segs)
                def _(s):
                    relay(f, h, s)

        @pl.loop(0, segs)
        def _(s):
            part = rows_of(s)
            sums = acc[part, :]
            for f in far:
                took(twin_of(f), 2 * j, s)
                took(twin_of(f), 2 * j + 1, s)
                sums = sums + product(f, j, part) + product(twin_of(f), j, part)
            acc[part, :] = sums

    last = pairs - 1

    def close(s):
        part = rows_of(s)
        sums = acc[part, :]
        for f in far:
            took(twin_of(f), 2 * last, s)
            took(twin_of(f), 2 * last + 1, s)
            sums = sums + product(twin_of(f), last, part)
        out_ref[part, :] = sums.astype(BF16)

    @pl.loop(0, segs)
    def _(s):
        part = rows_of(s)
        for f in far:
            relay(f, 2 * last, s)
            relay(f, 2 * last + 1, s)
        sums = acc[part, :]
        for f in far:
            sums = sums + product(f, last, part)
        acc[part, :] = sums

        @pl.when(s > 0)
        def _():
            close(s - 1)

    close(segs - 1)

    for h in range(heads):
        x_copy(h).wait_send()

        @pl.loop(z + 1, zs)
        def _(t):
            z_copy(z, t, h).wait_send()

        @pl.loop(0, segs)
        def _(s):
            for t in far + [pair_h]:
                ctx_copy(me_h, t, h, s, c_send.at[t, h, s]).wait_send()
            for f in far:
                ctx_copy(f, pair_h, h, s, f_send.at[f, h, s]).wait_send()


def body(ns, nh, queries, keys, values, gate_bias, out_weight):
    rows, cols = queries.shape
    depth, outs = out_weight.shape
    segs, heads = rows // SEG, cols // DH
    zs = ns // 2
    hbm = pl.BlockSpec(memory_space=pl.ANY)
    dma = pltpu.SemaphoreType.DMA
    held = pltpu.VMEM((heads, rows, DH), BF16)
    mem = pltpu.VMEM((heads, MEM, DH), F32)
    sent = pltpu.VMEM((heads, SENT, DH), BF16)
    return pl.pallas_call(
        functools.partial(kernel, ns, nh),
        out_shape=pltpu.VMEM((rows, outs), BF16),
        in_specs=[hbm, hbm, hbm, pl.BlockSpec(memory_space=pltpu.SMEM), hbm],
        out_specs=pl.BlockSpec(memory_space=pltpu.VMEM),
        scratch_shapes=[
            held, held, held,
            pltpu.VMEM((depth, outs), BF16),
            pltpu.VMEM((heads, rows, DH), F32),
            pltpu.VMEM((heads, segs, MEM, DH), F32),
            mem, sent, sent, sent,
            pltpu.VMEM((zs, heads, SENT, DH), BF16),
            mem,
            pltpu.VMEM((nh * heads, rows, DH), BF16),
            pltpu.VMEM((rows, outs), F32),
            dma((3, heads)), dma, dma((heads,)), dma((heads,)), dma((zs, heads)), dma((zs, heads)),
            dma((nh, heads, segs)), dma((nh, heads, segs)), dma((nh, heads, segs)),
        ],
        compiler_params=pltpu.CompilerParams(
            collective_id=0, has_side_effects=True, vmem_limit_bytes=56 * 1024 * 1024
        ),
        name="infini_layer",
    )(queries, keys, values, gate_bias, out_weight)


def solution(mesh):
    sizes = dict(mesh.shape)
    return jax.shard_map(
        functools.partial(body, sizes["seq"], sizes["head"]),
        mesh=mesh,
        in_specs=(P("seq", "head"), P("seq", "head"), P("seq", "head"), P("head"), P(None, "head")),
        out_specs=P("seq", "head"),
        check_vma=False,
    )
```

time: 49.6 us -> 40.7 us (0.82)
  the two profiles are of different devices: /device:TPU:25 before, /device:TPU:17 now
where the time goes in v2:
time: 40.7 us; the launch traced here: 40.6 us
  Pallas kernels  39.2 us (96%)
  local copies, waits for them, and re-layouts  1.32 us (3%)
    pallas_call x1, Pallas kernels, body(): pl.pallas_call(functools.partial(kernel, ns, nh), out_shape=pltpu.VMEM((r...  39.2 us
    unnamed x1, local copies, waits for them, and re-layouts  1.32 us

profile of v2, /device:TPU:17, one launch (start us, length us, event | category | flops | bytes accessed | tf_op | source)
XLA Modules:
  0.0 40.6 jit_solution(18441038109871756733)
XLA Ops:
  0.0 39.2 %infini_layer.1 = bf16[1024,1024]{1,0:T(8,128)(2,1)S(1)} custom-call(bf16[1024,512]{1,0:T(8,128)(2,1)} %q_hbm.1, bf16[1024,512]{1,0:T(8,128)(2,1)} %k_hbm.1, bf16[1024,512]{1,0:T(8,128)(2,1)} %v_hbm.1, f32[4]{0:T(128)} %gate_ref.1, bf16[2048,1024]{1,0:T(8,128)(2,1)} %w_hbm.1), custom_call_target="tpu_custom_call" | custom-call | tf_op jit(solution)/shard_map/infini_layer/pallas_call | solution.py:297
  39.3 1.3 %copy.7 = bf16[1024,1024]{1,0:T(8,128)(2,1)} copy(bf16[1024,1024]{1,0:T(8,128)(2,1)S(1)} %infini_layer.1) | data formatting | bytes 4194304

commit v3 on v2

v3 whole, which is shorter than its diff:
```python
import functools

import jax
import jax.numpy as jnp
from jax import lax
from jax.experimental import pallas as pl
from jax.experimental.pallas import tpu as pltpu
from jax.sharding import PartitionSpec as P

DH = 128
SEG = 256
MEM = DH + 8
SENT = DH + 16
EARLY = 2
MEET_FIRST = 4
MEET_GAP = 4
MEET_CORE = 0
MIX_FIRST = 5
MIX_HOP = 3
MESH = pl.DeviceIdType.MESH
F32 = jnp.float32
BF16 = jnp.bfloat16
NT = (((1,), (1,)), ((), ()))
TN = (((0,), (0,)), ((), ()))


def elu1(x):
    return jnp.where(x > 0.0, x + 1.0, jnp.exp(jnp.minimum(x, 0.0)))


def rows_of(s):
    return pl.ds(pl.multiple_of(s * SEG, SEG), SEG)


def cols_of(h):
    return pl.ds(pl.multiple_of(h * DH, DH), DH)


def packed(mem):
    return jnp.concatenate([mem, mem[DH:]], axis=0).astype(BF16)


def recall_of(q, mem):
    mem = jnp.concatenate(
        [mem[:DH], jnp.broadcast_to(mem[DH : DH + 1], (DH, DH))], axis=0
    ).astype(BF16)
    q_map = elu1(q.astype(F32)).astype(BF16)
    both = lax.dot_general(q_map, mem, NT, preferred_element_type=F32)
    return both[:, :DH] / (both[:, DH:] + 1.0)


def kernel(
    ns, nh, q_hbm, k_hbm, v_hbm, gate_hbm, w_hbm, out_ref,
    q_ref, kv_ref, gate_ref, w_ref, local, inner, total, mine, from_pair, plane, from_plane, prior,
    ctx, acc, own_local, own_inner, own_prior, far_early,
    kv_sem, q_sem, gate_sem, w_sem, open_sem, x_send, x_recv, z_send, z_recv,
    pair_send, pair_recv, far_send, far_recv, twin_send, twin_recv, early_send, early_recv, late_recv,
):
    rows, cols = q_ref.shape
    segs, heads = rows // SEG, cols // DH
    pairs = heads // 2
    last = heads - 1
    blocks = segs * heads
    me_s, me_h = lax.axis_index("seq"), lax.axis_index("head")
    z, odd = me_s // 2, lax.rem(me_s, 2)
    zs = ns // 2
    pair_s = me_s + 1 - 2 * odd
    group, core = me_h // 2, lax.rem(me_h, 2)
    pair_h = me_h + 1 - 2 * core
    groups = nh // 2
    far = [lax.rem(group + d, groups) * 2 + core for d in range(1, groups)]
    twin = [lax.rem(group + d, groups) * 2 + 1 - core for d in range(1, groups)]

    def load(i, h):
        src = (k_hbm, v_hbm)[i]
        return pltpu.make_async_copy(src.at[:, cols_of(h)], kv_ref.at[h, i], kv_sem.at[h])

    def loaded(h):
        pltpu.make_async_copy(kv_ref.at[h], kv_ref.at[h], kv_sem.at[h]).wait()

    q_copy = pltpu.make_async_copy(q_hbm, q_ref, q_sem)
    gate_copy = pltpu.make_async_copy(gate_hbm, gate_ref, gate_sem)
    weight_copy = pltpu.make_async_copy(w_hbm, w_ref, w_sem)
    for h in range(heads):
        load(0, h).start()
        load(1, h).start()
    q_copy.start()
    gate_copy.start()
    weight_copy.start()

    barrier = pltpu.get_barrier_semaphore()
    pl.semaphore_signal(barrier, inc=1, device_id=(pair_s, me_h), device_id_type=MESH)
    for h in [pair_h] + far:
        pl.semaphore_signal(barrier, inc=1, device_id=(me_s, h), device_id_type=MESH)

    @pl.loop(z + 1, zs)
    def _(t):
        pl.semaphore_signal(barrier, inc=1, device_id=(t * 2 + odd, me_h), device_id_type=MESH)

    pl.semaphore_wait(barrier, 2 + len(far) + z)

    @pl.loop(0, z)
    def _(p):
        pl.semaphore_signal(open_sem, inc=1, device_id=(p * 2 + odd, me_h), device_id_type=MESH)

    def x_copy(h):
        return pltpu.make_async_remote_copy(
            src_ref=mine.at[h], dst_ref=from_pair.at[h],
            send_sem=x_send, recv_sem=x_recv.at[h],
            device_id=(pair_s, me_h), device_id_type=MESH,
        )

    def z_copy(source, target, h):
        return pltpu.make_async_remote_copy(
            src_ref=plane.at[h], dst_ref=from_plane.at[source, h],
            send_sem=z_send.at[target - source - 1], recv_sem=z_recv.at[source, h],
            device_id=(target * 2 + odd, me_h), device_id_type=MESH,
        )

    def to_head(part, target, send, recv):
        return pltpu.make_async_remote_copy(
            src_ref=part, dst_ref=part, send_sem=send, recv_sem=recv,
            device_id=(me_s, target), device_id_type=MESH,
        )

    def to_pair(part):
        return to_head(part, pair_h, pair_send, pair_recv)

    def to_far(d, part, unit):
        return to_head(part, far[d], far_send.at[d, unit], far_recv.at[groups - 2 - d, unit])

    def from_far(d, part, unit):
        return to_head(part, far[d], far_send.at[d, unit], far_recv.at[d, unit])

    def relay(d, part, unit):
        return to_head(part, pair_h, twin_send.at[d], twin_recv.at[d, unit])

    early_rows = pl.ds(0, EARLY * SEG)
    q_at, local_at, inner_at = 0, EARLY * SEG, 2 * EARLY * SEG
    prior_at = inner_at + (EARLY - 1) * SENT

    def early(d, src, at, recv):
        slot = groups - 2 - d
        return pltpu.make_async_remote_copy(
            src_ref=src, dst_ref=far_early.at[slot, pl.ds(at, src.shape[0])],
            send_sem=early_send.at[d], recv_sem=recv.at[slot],
            device_id=(me_s, far[d]), device_id_type=MESH,
        )

    def early_done(d, at, size, sem):
        part = far_early.at[d, pl.ds(at, size)]
        return to_head(part, far[d], early_send.at[d], sem.at[d])

    def gate_of(h):
        return 1.0 / (1.0 + jnp.exp(-jnp.full((1, DH), gate_ref[h], F32)))

    def gated(mem):
        return packed(jnp.concatenate([gate_of(last) * mem[:DH], mem[DH:]], axis=0))

    for h in range(heads):
        loaded(h)
        run = jnp.zeros((MEM, DH), F32)
        for s in range(segs):
            inner[h, s] = run
            part = pl.ds(s * SEG, SEG)
            key_map = elu1(kv_ref[h, 0, part].astype(F32)).astype(BF16)
            delta = lax.dot_general(kv_ref[h, 1, part], key_map, TN, preferred_element_type=F32)
            norm = jnp.sum(key_map.astype(F32), axis=0, keepdims=True)
            run = run + jnp.concatenate([delta, jnp.broadcast_to(norm, (8, DH))], axis=0)
        total[h] = run
        mine[h] = packed(run)
        x_copy(h).start()
        if h == min(1, last):
            q_copy.wait()
            for d in range(len(far)):
                early(d, q_ref.at[early_rows, cols_of(last)], q_at, early_recv).start()

    gate_copy.wait()
    for s in range(1, EARLY):
        own_inner[pl.ds((s - 1) * SENT, SENT)] = gated(inner[last, s])
    for d in range(len(far)):
        early(d, own_inner, inner_at, early_recv).start()

    def meet(h):
        x_copy(h).wait_recv()
        other = from_pair[h].astype(F32)[:MEM]
        plane[h] = packed(total[h] + other)
        if h == 0:
            @pl.when(z < zs - 1)
            def _():
                pl.semaphore_wait(open_sem, zs - 1 - z)

        @pl.loop(0, zs - 1 - z)
        def _(t):
            z_copy(z, zs - 1 - t, h).start()

        prior[h] = jnp.where(odd == 1, other, 0.0)

    def mix(h, s):
        part = rows_of(s)
        gate = gate_of(h)
        recall = recall_of(q_ref[part, cols_of(h)], prior[h] + inner[h, s])
        ctx[me_h * heads + h, part] = (gate * recall + (1.0 - gate) * local[h, part]).astype(BF16)

    def send_one(h, s, unit):
        part = ctx.at[me_h * heads + h, rows_of(s)]
        for d in range(len(far)):
            to_far(d, part, unit).start()

    def arrive(h):
        @pl.loop(0, z)
        def _(p):
            z_copy(p, z, h).wait_recv()
            prior[h] = prior[h] + from_plane[p, h].astype(F32)[:MEM]

    def both_of(source, s):
        return ctx.at[pl.ds(source * heads + last - 1, 2), rows_of(s)]

    def finish(c):
        arrive(c)
        if c < last - 1:
            @pl.loop(0, segs)
            def _(s):
                mix(c, s)
                send_one(c, s, c)
                to_pair(ctx.at[me_h * heads + c, rows_of(s)]).start()
        elif c == last:
            own_prior[...] = gated(prior[last])
            for d in range(len(far)):
                early(d, own_prior, prior_at, late_recv).start()

            @pl.loop(0, segs)
            def _(s):
                mix(last - 1, s)

                @pl.when(s < EARLY)
                def _():
                    send_one(last - 1, s, last - 1 + s)

                mix(last, s)

                @pl.when(s >= EARLY)
                def _():
                    for d in range(len(far)):
                        to_far(d, both_of(me_h, s), last - 1 + s).start()

                to_pair(both_of(me_h, s)).start()

    row_id = lax.broadcasted_iota(jnp.int32, (SEG, SEG), 0)
    col_id = lax.broadcasted_iota(jnp.int32, (SEG, SEG), 1)
    ones = jnp.ones((SEG, DH), BF16)

    def attend(h, s):
        part = rows_of(s)
        scores = lax.dot_general(
            q_ref[part, cols_of(h)], kv_ref[h, 0, part], NT, preferred_element_type=F32
        )
        scores = jnp.where(row_id >= col_id, scores * (1.0 / DH**0.5), -1e30)
        weights = jnp.exp(scores - jnp.max(scores, axis=1, keepdims=True)).astype(BF16)
        both = jnp.dot(
            weights, jnp.concatenate([kv_ref[h, 1, part], ones], axis=1), preferred_element_type=F32
        )
        local[h, part] = both[:, :DH] / both[:, DH:]

    def send_local():
        own_local[...] = ((1.0 - gate_of(last)) * local[last, early_rows]).astype(BF16)
        for d in range(len(far)):
            early(d, own_local, local_at, early_recv).start()

    def meet_at(c):
        return MEET_FIRST + MEET_CORE * core + MEET_GAP * c

    def finish_at(c):
        done = segs if c == 0 else blocks if c == last else EARLY + segs * (c + 1)
        ready = jnp.maximum(MIX_FIRST + MIX_HOP * jnp.minimum(z, 2) + c, meet_at(c) + 1)
        return jnp.maximum(ready, done)

    @pl.loop(0, blocks)
    def _(b):
        for c in range(heads):
            @pl.when(b == meet_at(c))
            def _():
                meet(c)
        for c in range(heads):
            @pl.when(b == finish_at(c))
            def _():
                finish(c)

        @pl.when(b == segs + EARLY)
        def _():
            send_local()

        first = last * segs
        i = jnp.where(b < segs, b, jnp.where(b < segs + EARLY, b - segs + first, jnp.where(b < first + EARLY, b - EARLY, b)))
        attend(i // segs, lax.rem(i, segs))

    for c in range(heads):
        @pl.when(meet_at(c) >= blocks)
        def _():
            meet(c)
    for c in range(heads):
        @pl.when(finish_at(c) >= blocks)
        def _():
            finish(c)

    weight_copy.wait()

    def product(source, j, part):
        slot = source * heads + 2 * j
        return jnp.dot(
            jnp.concatenate([ctx[slot, part], ctx[slot + 1, part]], axis=1),
            w_ref[pl.ds(pl.multiple_of(slot * DH, 2 * DH), 2 * DH), :],
            preferred_element_type=F32,
        )

    to_pair(ctx.at[pl.ds(pair_h * heads, heads)]).wait_recv()

    @pl.loop(0, segs)
    def _(s):
        part = rows_of(s)
        sums = product(me_h, 0, part)
        for j in range(1, pairs):
            sums = sums + product(me_h, j, part)
        for j in range(pairs):
            sums = sums + product(pair_h, j, part)
        acc[part, :] = sums

    for j in range(pairs - 1):
        for d in range(len(far)):
            for h in (2 * j, 2 * j + 1):
                whole = ctx.at[far[d] * heads + h]
                from_far(d, whole, h).wait_recv()
                relay(d, whole, j).start()
        for d in range(len(far)):
            relay(d, ctx.at[pl.ds(twin[d] * heads + 2 * j, 2)], j).wait_recv()

        @pl.loop(0, segs)
        def _(s):
            part = rows_of(s)
            sums = acc[part, :]
            for d in range(len(far)):
                sums = sums + product(far[d], j, part) + product(twin[d], j, part)
            acc[part, :] = sums

    for d in range(len(far)):
        early_done(d, 0, prior_at, early_recv).wait_recv()
        early_done(d, prior_at, SENT, late_recv).wait_recv()
        for s in range(EARLY):
            mem = far_early[d, pl.ds(prior_at, SENT)].astype(F32)[:MEM]
            if s > 0:
                mem = mem + far_early[d, pl.ds(inner_at + (s - 1) * SENT, SENT)].astype(F32)[:MEM]
            value = recall_of(far_early[d, pl.ds(q_at + s * SEG, SEG)], mem)
            value = value + far_early[d, pl.ds(local_at + s * SEG, SEG)].astype(F32)
            ctx[far[d] * heads + last, pl.ds(s * SEG, SEG)] = value.astype(BF16)

    def close(s):
        part = rows_of(s)
        sums = acc[part, :]
        for d in range(len(far)):
            relay(d, both_of(twin[d], s), pairs - 1 + s).wait_recv()
            sums = sums + product(twin[d], pairs - 1, part)
        out_ref[part, :] = sums.astype(BF16)

    @pl.loop(0, segs)
    def _(s):
        part = rows_of(s)
        for d in range(len(far)):
            @pl.when(s < EARLY)
            def _():
                from_far(d, ctx.at[far[d] * heads + last - 1, part], last - 1 + s).wait_recv()

            @pl.when(s >= EARLY)
            def _():
                from_far(d, both_of(far[d], s), last - 1 + s).wait_recv()

            relay(d, both_of(far[d], s), pairs - 1 + s).start()
        sums = acc[part, :]
        for d in range(len(far)):
            sums = sums + product(far[d], pairs - 1, part)
        acc[part, :] = sums

        @pl.when(s > 0)
        def _():
            close(s - 1)

    pltpu.make_async_remote_copy(
        src_ref=mine, dst_ref=mine, send_sem=x_send, recv_sem=x_recv.at[0],
        device_id=(pair_s, me_h), device_id_type=MESH,
    ).wait_send()

    @pl.loop(z + 1, zs)
    def _(t):
        pltpu.make_async_remote_copy(
            src_ref=plane, dst_ref=plane, send_sem=z_send.at[t - z - 1], recv_sem=z_recv.at[0, 0],
            device_id=(t * 2 + odd, me_h), device_id_type=MESH,
        ).wait_send()

    to_pair(ctx.at[pl.ds(me_h * heads, heads)]).wait_send()
    for d in range(len(far)):
        for h in range(last - 1):
            to_far(d, ctx.at[me_h * heads + h], h).wait_send()
        for s in range(segs):
            part = both_of(me_h, s) if s >= EARLY else ctx.at[me_h * heads + last - 1, rows_of(s)]
            to_far(d, part, last - 1 + s).wait_send()
        early_done(d, 0, prior_at + SENT, early_recv).wait_send()

    close(segs - 1)
    for d in range(len(far)):
        relay(d, ctx.at[pl.ds(far[d] * heads, heads)], 0).wait_send()


def body(ns, nh, queries, keys, values, gate_bias, out_weight):
    rows, cols = queries.shape
    depth, outs = out_weight.shape
    segs, heads = rows // SEG, cols // DH
    pairs = heads // 2
    zs = ns // 2
    fars = nh // 2 - 1
    hbm = pl.BlockSpec(memory_space=pl.ANY)
    dma = pltpu.SemaphoreType.DMA
    mem = pltpu.VMEM((heads, MEM, DH), F32)
    sent = pltpu.VMEM((heads, SENT, DH), BF16)
    return pl.pallas_call(
        functools.partial(kernel, ns, nh),
        out_shape=pltpu.VMEM((rows, outs), BF16),
        in_specs=[hbm, hbm, hbm, hbm, hbm],
        out_specs=pl.BlockSpec(memory_space=pltpu.VMEM),
        scratch_shapes=[
            pltpu.VMEM((rows, cols), BF16),
            pltpu.VMEM((heads, 2, rows, DH), BF16),
            pltpu.SMEM((heads,), F32),
            pltpu.VMEM((depth, outs), BF16),
            pltpu.VMEM((heads, rows, DH), F32),
            pltpu.VMEM((heads, segs, MEM, DH), F32),
            mem, sent, sent, sent,
            pltpu.VMEM((zs - 1, heads, SENT, DH), BF16),
            mem,
            pltpu.VMEM((nh * heads, rows, DH), BF16),
            pltpu.VMEM((rows, outs), F32),
            pltpu.VMEM((EARLY * SEG, DH), BF16),
            pltpu.VMEM(((EARLY - 1) * SENT, DH), BF16),
            pltpu.VMEM((SENT, DH), BF16),
            pltpu.VMEM((fars, 2 * EARLY * SEG + EARLY * SENT, DH), BF16),
            dma((heads,)), dma, dma, dma, pltpu.SemaphoreType.REGULAR,
            dma, dma((heads,)), dma((zs - 1,)), dma((zs - 1, heads)),
            dma, dma, dma((fars, heads - 2 + segs)), dma((fars, heads - 2 + segs)),
            dma((fars,)), dma((fars, pairs - 1 + segs)),
            dma((fars,)), dma((fars,)), dma((fars,)),
        ],
        compiler_params=pltpu.CompilerParams(
            collective_id=0, has_side_effects=True, vmem_limit_bytes=56 * 1024 * 1024
        ),
        name="infini_layer",
    )(queries, keys, values, gate_bias, out_weight)


def solution(mesh):
    sizes = dict(mesh.shape)
    return jax.shard_map(
        functools.partial(body, sizes["seq"], sizes["head"]),
        mesh=mesh,
        in_specs=(P("seq", "head"), P("seq", "head"), P("seq", "head"), P("head"), P(None, "head")),
        out_specs=P("seq", "head"),
        check_vma=False,
    )
```

time: 40.7 us -> 36.5 us (0.90)
  the two profiles are of different devices: /device:TPU:17 before, /device:TPU:25 now
where the time goes in v3:
time: 36.5 us; the launch traced here: 36.3 us
  Pallas kernels  35 us (96%)
  local copies, waits for them, and re-layouts  1.32 us (4%)
    pallas_call x1, Pallas kernels, body(): pl.pallas_call(functools.partial(kernel, ns, nh), out_shape=pltpu.VMEM((r...  35 us
    unnamed x1, local copies, waits for them, and re-layouts  1.32 us

profile of v3, /device:TPU:25, one launch (start us, length us, event | category | flops | bytes accessed | tf_op | source)
XLA Modules:
  0.0 36.3 jit_solution(14338152460054347802)
XLA Ops:
  0.0 35.0 %infini_layer.1 = bf16[1024,1024]{1,0:T(8,128)(2,1)S(1)} custom-call(bf16[1024,512]{1,0:T(8,128)(2,1)} %q_hbm.1, bf16[1024,512]{1,0:T(8,128)(2,1)} %k_hbm.1, bf16[1024,512]{1,0:T(8,128)(2,1)} %v_hbm.1, f32[4]{0:T(128)} %gate_hbm.1, bf16[2048,1024]{1,0:T(8,128)(2,1)} %w_hbm.1), custom_call_target="tpu_custom_call" | custom-call | tf_op jit(solution)/shard_map/infini_layer/pallas_call | solution.py:423
  35.0 1.3 %copy.7 = bf16[1024,1024]{1,0:T(8,128)(2,1)} copy(bf16[1024,1024]{1,0:T(8,128)(2,1)S(1)} %infini_layer.1) | data formatting | bytes 4194304

commit v4 on v3

--- a/solution.py
+++ b/solution.py
@@ -13,7 +13,7 @@
 SENT = DH + 16
 EARLY = 2
 MEET_FIRST = 4
-MEET_GAP = 4
+MEET_GAP = 5
 MEET_CORE = 0
 MIX_FIRST = 5
 MIX_HOP = 3
@@ -68,6 +68,7 @@
     group, core = me_h // 2, lax.rem(me_h, 2)
     pair_h = me_h + 1 - 2 * core
     groups = nh // 2
+    ahead = z > 0
     far = [lax.rem(group + d, groups) * 2 + core for d in range(1, groups)]
     twin = [lax.rem(group + d, groups) * 2 + 1 - core for d in range(1, groups)]
 
@@ -123,8 +124,8 @@
             device_id=(me_s, target), device_id_type=MESH,
         )
 
-    def to_pair(part):
-        return to_head(part, pair_h, pair_send, pair_recv)
+    def to_pair(part, j):
+        return to_head(part, pair_h, pair_send, pair_recv.at[j])
 
     def to_far(d, part, unit):
         return to_head(part, far[d], far_send.at[d, unit], far_recv.at[groups - 2 - d, unit])
@@ -172,14 +173,20 @@
         x_copy(h).start()
         if h == min(1, last):
             q_copy.wait()
-            for d in range(len(far)):
-                early(d, q_ref.at[early_rows, cols_of(last)], q_at, early_recv).start()
+
+            @pl.when(ahead)
+            def _():
+                for d in range(len(far)):
+                    early(d, q_ref.at[early_rows, cols_of(last)], q_at, early_recv).start()
 
     gate_copy.wait()
-    for s in range(1, EARLY):
-        own_inner[pl.ds((s - 1) * SENT, SENT)] = gated(inner[last, s])
-    for d in range(len(far)):
-        early(d, own_inner, inner_at, early_recv).start()
+
+    @pl.when(ahead)
+    def _():
+        for s in range(1, EARLY):
+            own_inner[pl.ds((s - 1) * SENT, SENT)] = gated(inner[last, s])
+        for d in range(len(far)):
+            early(d, own_inner, inner_at, early_recv).start()
 
     def meet(h):
         x_copy(h).wait_recv()
@@ -192,7 +199,7 @@
 
         @pl.loop(0, zs - 1 - z)
         def _(t):
-            z_copy(z, zs - 1 - t, h).start()
+            z_copy(z, jnp.where(z == 0, zs - 1 - t, z + 1 + t), h).start()
 
         prior[h] = jnp.where(odd == 1, other, 0.0)
 
@@ -223,28 +230,32 @@
             def _(s):
                 mix(c, s)
                 send_one(c, s, c)
-                to_pair(ctx.at[me_h * heads + c, rows_of(s)]).start()
+                to_pair(ctx.at[me_h * heads + c, rows_of(s)], c // 2).start()
         elif c == last:
-            own_prior[...] = gated(prior[last])
-            for d in range(len(far)):
-                early(d, own_prior, prior_at, late_recv).start()
+            @pl.when(ahead)
+            def _():
+                own_prior[...] = gated(prior[last])
+                for d in range(len(far)):
+                    early(d, own_prior, prior_at, late_recv).start()
 
             @pl.loop(0, segs)
             def _(s):
                 mix(last - 1, s)
 
-                @pl.when(s < EARLY)
+                alone = jnp.logical_and(ahead, s < EARLY)
+
+                @pl.when(alone)
                 def _():
                     send_one(last - 1, s, last - 1 + s)
 
                 mix(last, s)
 
-                @pl.when(s >= EARLY)
+                @pl.when(jnp.logical_not(alone))
                 def _():
                     for d in range(len(far)):
                         to_far(d, both_of(me_h, s), last - 1 + s).start()
 
-                to_pair(both_of(me_h, s)).start()
+                to_pair(both_of(me_h, s), pairs - 1).start()
 
     row_id = lax.broadcasted_iota(jnp.int32, (SEG, SEG), 0)
     col_id = lax.broadcasted_iota(jnp.int32, (SEG, SEG), 1)
@@ -273,7 +284,8 @@
     def finish_at(c):
         done = segs if c == 0 else blocks if c == last else EARLY + segs * (c + 1)
         ready = jnp.maximum(MIX_FIRST + MIX_HOP * jnp.minimum(z, 2) + c, meet_at(c) + 1)
-        return jnp.maximum(ready, done)
+        ready = jnp.maximum(ready, done)
+        return ready if c == 0 else jnp.where(ahead, blocks, ready)
 
     @pl.loop(0, blocks)
     def _(b):
@@ -281,12 +293,12 @@
             @pl.when(b == meet_at(c))
             def _():
                 meet(c)
-        for c in range(heads):
+        for c in range(last - 1):
             @pl.when(b == finish_at(c))
             def _():
                 finish(c)
 
-        @pl.when(b == segs + EARLY)
+        @pl.when(jnp.logical_and(ahead, b == segs + EARLY))
         def _():
             send_local()
 
@@ -298,7 +310,7 @@
         @pl.when(meet_at(c) >= blocks)
         def _():
             meet(c)
-    for c in range(heads):
+    for c in range(last - 1):
         @pl.when(finish_at(c) >= blocks)
         def _():
             finish(c)
@@ -313,17 +325,18 @@
             preferred_element_type=F32,
         )
 
-    to_pair(ctx.at[pl.ds(pair_h * heads, heads)]).wait_recv()
-
-    @pl.loop(0, segs)
-    def _(s):
-        part = rows_of(s)
-        sums = product(me_h, 0, part)
-        for j in range(1, pairs):
-            sums = sums + product(me_h, j, part)
-        for j in range(pairs):
-            sums = sums + product(pair_h, j, part)
-        acc[part, :] = sums
+    def pair_of(source, j):
+        return ctx.at[pl.ds(source * heads + 2 * j, 2)]
+
+    for j in range(pairs - 1):
+        to_pair(pair_of(pair_h, j), j).wait_recv()
+        for s in range(segs):
+            part = rows_of(s)
+            sums = product(me_h, j, part) + product(pair_h, j, part)
+            acc[part, :] = sums if j == 0 else acc[part, :] + sums
+
+    finish(last - 1)
+    finish(last)
 
     for j in range(pairs - 1):
         for d in range(len(far)):
@@ -331,18 +344,8 @@
                 whole = ctx.at[far[d] * heads + h]
                 from_far(d, whole, h).wait_recv()
                 relay(d, whole, j).start()
-        for d in range(len(far)):
-            relay(d, ctx.at[pl.ds(twin[d] * heads + 2 * j, 2)], j).wait_recv()
-
-        @pl.loop(0, segs)
-        def _(s):
-            part = rows_of(s)
-            sums = acc[part, :]
-            for d in range(len(far)):
-                sums = sums + product(far[d], j, part) + product(twin[d], j, part)
-            acc[part, :] = sums
-
-    for d in range(len(far)):
+
+    def cross(d):
         early_done(d, 0, prior_at, early_recv).wait_recv()
         early_done(d, prior_at, SENT, late_recv).wait_recv()
         for s in range(EARLY):
@@ -353,35 +356,62 @@
             value = value + far_early[d, pl.ds(local_at + s * SEG, SEG)].astype(F32)
             ctx[far[d] * heads + last, pl.ds(s * SEG, SEG)] = value.astype(BF16)
 
-    def close(s):
+    def take(s):
+        for d in range(len(far)):
+            two = both_of(far[d], s)
+            if s < EARLY:
+                @pl.when(ahead)
+                def _():
+                    one = ctx.at[far[d] * heads + last - 1, rows_of(s)]
+                    from_far(d, one, last - 1 + s).wait_recv()
+
+                @pl.when(jnp.logical_not(ahead))
+                def _():
+                    from_far(d, two, last - 1 + s).wait_recv()
+            else:
+                from_far(d, two, last - 1 + s).wait_recv()
+            relay(d, two, pairs - 1 + s).start()
+
+    def twins(s):
+        for d in range(len(far)):
+            relay(d, both_of(twin[d], s), pairs - 1 + s).wait_recv()
+
+    def tail(sources, s):
+        sums = acc[rows_of(s), :]
+        for source in sources:
+            sums = sums + product(source, pairs - 1, rows_of(s))
+        return sums
+
+    def fill(s):
         part = rows_of(s)
-        sums = acc[part, :]
-        for d in range(len(far)):
-            relay(d, both_of(twin[d], s), pairs - 1 + s).wait_recv()
-            sums = sums + product(twin[d], pairs - 1, part)
-        out_ref[part, :] = sums.astype(BF16)
-
-    @pl.loop(0, segs)
-    def _(s):
-        part = rows_of(s)
-        for d in range(len(far)):
-            @pl.when(s < EARLY)
+        sums = product(me_h, pairs - 1, part) + product(pair_h, pairs - 1, part)
+        for j in range(pairs - 1):
+            for d in range(len(far)):
+                sums = sums + product(far[d], j, part) + product(twin[d], j, part)
+        acc[part, :] = acc[part, :] + sums if pairs > 1 else sums
+
+    to_pair(pair_of(pair_h, pairs - 1), pairs - 1).wait_recv()
+    for j in range(pairs - 1):
+        for d in range(len(far)):
+            relay(d, pair_of(twin[d], j), j).wait_recv()
+    for s in range(segs):
+        if s == min(1, segs - 1):
+            @pl.when(ahead)
             def _():
-                from_far(d, ctx.at[far[d] * heads + last - 1, part], last - 1 + s).wait_recv()
-
-            @pl.when(s >= EARLY)
-            def _():
-                from_far(d, both_of(far[d], s), last - 1 + s).wait_recv()
-
-            relay(d, both_of(far[d], s), pairs - 1 + s).start()
-        sums = acc[part, :]
-        for d in range(len(far)):
-            sums = sums + product(far[d], pairs - 1, part)
-        acc[part, :] = sums
-
-        @pl.when(s > 0)
-        def _():
-            close(s - 1)
+                for d in range(len(far)):
+                    cross(d)
+        if 0 < s <= EARLY:
+            take(s - 1)
+        fill(s)
+    for s in range(EARLY):
+        twins(s)
+        out_ref[rows_of(s), :] = tail(far + twin, s).astype(BF16)
+    for s in range(EARLY, segs - 1):
+        take(s)
+        twins(s)
+        out_ref[rows_of(s), :] = tail(far + twin, s).astype(BF16)
+    take(segs - 1)
+    acc[rows_of(segs - 1), :] = tail(far, segs - 1)
 
     pltpu.make_async_remote_copy(
         src_ref=mine, dst_ref=mine, send_sem=x_send, recv_sem=x_recv.at[0],
@@ -395,16 +425,27 @@
             device_id=(t * 2 + odd, me_h), device_id_type=MESH,
         ).wait_send()
 
-    to_pair(ctx.at[pl.ds(me_h * heads, heads)]).wait_send()
+    to_pair(ctx.at[pl.ds(me_h * heads, heads)], 0).wait_send()
     for d in range(len(far)):
         for h in range(last - 1):
             to_far(d, ctx.at[me_h * heads + h], h).wait_send()
-        for s in range(segs):
-            part = both_of(me_h, s) if s >= EARLY else ctx.at[me_h * heads + last - 1, rows_of(s)]
-            to_far(d, part, last - 1 + s).wait_send()
-        early_done(d, 0, prior_at + SENT, early_recv).wait_send()
-
-    close(segs - 1)
+        for s in range(EARLY, segs):
+            to_far(d, both_of(me_h, s), last - 1 + s).wait_send()
+
+        @pl.when(ahead)
+        def _():
+            for s in range(EARLY):
+                one = ctx.at[me_h * heads + last - 1, rows_of(s)]
+                to_far(d, one, last - 1 + s).wait_send()
+            early_done(d, 0, prior_at + SENT, early_recv).wait_send()
+
+        @pl.when(jnp.logical_not(ahead))
+        def _():
+            for s in range(EARLY):
+                to_far(d, both_of(me_h, s), last - 1 + s).wait_send()
+
+    twins(segs - 1)
+    out_ref[rows_of(segs - 1), :] = tail(twin, segs - 1).astype(BF16)
     for d in range(len(far)):
         relay(d, ctx.at[pl.ds(far[d] * heads, heads)], 0).wait_send()
 
@@ -443,7 +484,7 @@
             pltpu.VMEM((fars, 2 * EARLY * SEG + EARLY * SENT, DH), BF16),
             dma((heads,)), dma, dma, dma, pltpu.SemaphoreType.REGULAR,
             dma, dma((heads,)), dma((zs - 1,)), dma((zs - 1, heads)),
-            dma, dma, dma((fars, heads - 2 + segs)), dma((fars, heads - 2 + segs)),
+            dma, dma((pairs,)), dma((fars, heads - 2 + segs)), dma((fars, heads - 2 + segs)),
             dma((fars,)), dma((fars, pairs - 1 + segs)),
             dma((fars,)), dma((fars,)), dma((fars,)),
         ],

time: 36.5 us -> 35.2 us (0.964)
  Pallas kernels: 35 us -> 33.4 us
    pallas_call x1, Pallas kernels: 35 us -> 33.4 us  [body(): pl.pallas_call(functools.partial(kernel, ns, nh), out_shape=pltpu.VMEM((r...]
where the time goes in v4:
time: 35.2 us; the launch traced here: 34.7 us
  Pallas kernels  33.4 us (95%)
  local copies, waits for them, and re-layouts  1.32 us (4%)
    pallas_call x1, Pallas kernels, body(): pl.pallas_call(functools.partial(kernel, ns, nh), out_shape=pltpu.VMEM((r...  33.4 us
    unnamed x1, local copies, waits for them, and re-layouts  1.32 us

profile of v4, /device:TPU:25, one launch (start us, length us, event | category | flops | bytes accessed | tf_op | source)
XLA Modules:
  0.0 34.7 jit_solution(9694731893043774561)
XLA Ops:
  0.0 33.4 %infini_layer.1 = bf16[1024,1024]{1,0:T(8,128)(2,1)S(1)} custom-call(bf16[1024,512]{1,0:T(8,128)(2,1)} %q_hbm.1, bf16[1024,512]{1,0:T(8,128)(2,1)} %k_hbm.1, bf16[1024,512]{1,0:T(8,128)(2,1)} %v_hbm.1, f32[4]{0:T(128)} %gate_hbm.1, bf16[2048,1024]{1,0:T(8,128)(2,1)} %w_hbm.1), custom_call_target="tpu_custom_call" | custom-call | tf_op jit(solution)/shard_map/infini_layer/pallas_call | solution.py:464
  33.4 1.3 %copy.7 = bf16[1024,1024]{1,0:T(8,128)(2,1)} copy(bf16[1024,1024]{1,0:T(8,128)(2,1)S(1)} %infini_layer.1) | data formatting | bytes 4194304

commit v5 on v4

--- a/solution.py
+++ b/solution.py
@@ -87,7 +87,6 @@
         load(1, h).start()
     q_copy.start()
     gate_copy.start()
-    weight_copy.start()
 
     barrier = pltpu.get_barrier_semaphore()
     pl.semaphore_signal(barrier, inc=1, device_id=(pair_s, me_h), device_id_type=MESH)
@@ -179,6 +178,7 @@
                 for d in range(len(far)):
                     early(d, q_ref.at[early_rows, cols_of(last)], q_at, early_recv).start()
 
+    weight_copy.start()
     gate_copy.wait()
 
     @pl.when(ahead)
@@ -329,10 +329,9 @@
         return ctx.at[pl.ds(source * heads + 2 * j, 2)]
 
     for j in range(pairs - 1):
-        to_pair(pair_of(pair_h, j), j).wait_recv()
         for s in range(segs):
             part = rows_of(s)
-            sums = product(me_h, j, part) + product(pair_h, j, part)
+            sums = product(me_h, j, part)
             acc[part, :] = sums if j == 0 else acc[part, :] + sums
 
     finish(last - 1)
@@ -386,11 +385,13 @@
         part = rows_of(s)
         sums = product(me_h, pairs - 1, part) + product(pair_h, pairs - 1, part)
         for j in range(pairs - 1):
+            sums = sums + product(pair_h, j, part)
             for d in range(len(far)):
                 sums = sums + product(far[d], j, part) + product(twin[d], j, part)
         acc[part, :] = acc[part, :] + sums if pairs > 1 else sums
 
-    to_pair(pair_of(pair_h, pairs - 1), pairs - 1).wait_recv()
+    for j in range(pairs):
+        to_pair(pair_of(pair_h, j), j).wait_recv()
     for j in range(pairs - 1):
         for d in range(len(far)):
             relay(d, pair_of(twin[d], j), j).wait_recv()

time: 35.2 us -> 35.2 us (level)
  no operation moved by 1% of the time
where the time goes in v5:
time: 35.2 us; the launch traced here: 34.7 us
  Pallas kernels  33.4 us (95%)
  local copies, waits for them, and re-layouts  1.32 us (4%)
    pallas_call x1, Pallas kernels, body(): pl.pallas_call(functools.partial(kernel, ns, nh), out_shape=pltpu.VMEM((r...  33.4 us
    unnamed x1, local copies, waits for them, and re-layouts  1.32 us

profile of v5, /device:TPU:25, one launch (start us, length us, event | category | flops | bytes accessed | tf_op | source)
XLA Modules:
  0.0 34.7 jit_solution(17934643582832427050)
XLA Ops:
  0.0 33.4 %infini_layer.1 = bf16[1024,1024]{1,0:T(8,128)(2,1)S(1)} custom-call(bf16[1024,512]{1,0:T(8,128)(2,1)} %q_hbm.1, bf16[1024,512]{1,0:T(8,128)(2,1)} %k_hbm.1, bf16[1024,512]{1,0:T(8,128)(2,1)} %v_hbm.1, f32[4]{0:T(128)} %gate_hbm.1, bf16[2048,1024]{1,0:T(8,128)(2,1)} %w_hbm.1), custom_call_target="tpu_custom_call" | custom-call | tf_op jit(solution)/shard_map/infini_layer/pallas_call | solution.py:465
  33.4 1.3 %copy.7 = bf16[1024,1024]{1,0:T(8,128)(2,1)} copy(bf16[1024,1024]{1,0:T(8,128)(2,1)S(1)} %infini_layer.1) | data formatting | bytes 4194304
